TPU v7x, 128 devices: a whole 4x4x4 slice. The times are simulated.
128 devices in a mesh: brick: 32 (over z, y, core), mode: 4 (over x).
Axes of the slice: x: 4, y: 4, z: 4, core: 2. Of those that a mesh axis runs over, the one named last changes fastest.
Arguments:
- coeffs: float32 [32768, 3072], P('brick', 'mode'), may hold values from -6 to 6
- weights: bfloat16 [2, 1536, 32, 1024], P(None, 'brick'), may hold values from -0.1875 to 0.1875
- owners: int32 [2, 1536, 1], P(None, 'brick'), may hold values from 0 to 31; in each aligned block of 48 rows (0 to 47, 48 to 95, ..., all dimensions but the last counted through in order) at most 2 rows name the same one
- offsets: int32 [2, 1536], P(None, 'brick'), may hold values from 0 to 7
- mode_basis: bfloat16 [2, 3072, 1024], P(None, 'mode'), may hold values from -0.109375 to 0.109375
- measured: float32 [2, 8192, 1024], P(None, ('brick', 'mode')), may hold values from -6 to 6
Outputs:
- coeffs_out: float32 [32768, 3072], P('brick', 'mode')
- residual: float32 [2, 8192, 1024], P(None, ('brick', 'mode'))
Inputs may be any that keep to these rules, and one draw needn't show every extreme that they name: `owners`: among the 48 entries of one brick in one view, no owner is named more than 2 times.
All inputs are finite; a program needn't handle non-finite values.
Results may differ from a plain program's by a relative error of at most 0.0098.
Values may be sent and summed in bfloat16 or wider, within the bound.
A program may use at most 128 MiB of HBM per device.

v0:
```python
import functools

import jax
import jax.numpy as jnp
from jax import lax
from jax.experimental import pallas as pl
from jax.experimental.pallas import tpu as pltpu
from jax.sharding import PartitionSpec as P

BLK_DEV = 8
LEARN_RATE = 0.2
BF = jnp.bfloat16
F32 = jnp.float32
MESH = pl.DeviceIdType.MESH


def dot(a, b):
    return jnp.dot(a, b, preferred_element_type=F32)


def slot_tables(owner_list, offset_list, peer_count, capacity):
    slots = owner_list.shape[0]
    order = jnp.arange(slots, dtype=jnp.int32)
    same = owner_list[:, None] == owner_list[None, :]
    earlier = jnp.sum((same & (order[None, :] < order[:, None])).astype(jnp.int32), 1)
    places = owner_list * capacity + earlier
    hits = places[None, :] == jnp.arange(peer_count * capacity, dtype=jnp.int32)[:, None]
    source = slots + jnp.sum(jnp.where(hits, order[None, :] - slots, 0), 1)
    labels = BLK_DEV + jnp.sum(jnp.where(hits, offset_list[None, :] - BLK_DEV, 0), 1)
    return source, places, labels


def kernel(
    peers,
    modes,
    cap,
    source,
    places,
    label_out,
    picked,
    coeffs_hbm,
    weights_hbm,
    basis_hbm,
    measured_hbm,
    coeffs_out,
    residual_out,
    coef,
    low,
    basis,
    weight,
    chunk,
    target,
    qsend,
    qrel,
    qrecv,
    pattern,
    qlow,
    proj,
    fsend,
    frecv,
    ray,
    bsend,
    brecv0,
    brecv1,
    back,
    back_t,
    change,
    select,
    gram,
    gpart,
    grecv,
    label_in,
    label_s,
    result,
    collected,
    load_sem,
    local_sem,
    gs_sem,
    gr_sem,
    ts_sem,
    tr_sem,
    qs_sem,
    qr_sem,
    as_sem,
    ar_sem,
    rs_sem,
    rr_sem,
    all_s,
    all_r,
):
    brecv = (brecv0, brecv1)
    brick, mode = lax.axis_index("brick"), lax.axis_index("mode")
    right, left, far = [lax.rem(mode + k, modes) for k in (1, modes - 1, 2)]
    views, entries, voxels = weights_hbm.shape
    slots, ray_block = proj.shape[0] - 1, proj.shape[1]
    here, bins = basis.shape[1], basis.shape[2]
    mine = bins // modes
    places_n = peers * cap
    rays = BLK_DEV * ray_block
    tile = min(256, voxels)
    half, hm = voxels // 2, mine // 2
    share = gpart.shape[0] // modes

    def aligned(i, n):
        return pl.ds(pl.multiple_of(i * n, n), n)

    def to_mode(src, dst, s, r, peer):
        copy = pltpu.make_async_remote_copy(
            src_ref=src, dst_ref=dst, send_sem=s, recv_sem=r,
            device_id={"mode": peer}, device_id_type=MESH,
        )
        copy.start()

    def await_bytes(ref, sem):
        pltpu.make_async_copy(ref, ref, sem).wait()

    def to_bricks(src_of, dst, index):
        def body(k, carry):
            peer = lax.rem(brick + k, peers)
            copy = pltpu.make_async_remote_copy(
                src_ref=src_of(peer), dst_ref=dst, send_sem=all_s.at[index],
                recv_sem=all_r.at[index], device_id={"brick": peer}, device_id_type=MESH,
            )
            copy.start()
            return carry

        lax.fori_loop(1, peers, body, 0)

    loads = [
        pltpu.make_async_copy(basis_hbm, basis, load_sem.at[0]),
        pltpu.make_async_copy(coeffs_hbm, coef, load_sem.at[1]),
        pltpu.make_async_copy(weights_hbm.at[0], weight.at[0], load_sem.at[2]),
        pltpu.make_async_copy(weights_hbm.at[1], weight.at[1], load_sem.at[3]),
    ]
    loads += [
        pltpu.make_async_copy(
            measured_hbm.at[:, :, pl.ds(m * mine, mine)], chunk.at[m], load_sem.at[4 + m]
        )
        for m in range(modes)
    ]
    for load in loads:
        load.start()
    barrier = pltpu.get_barrier_semaphore()

    def greet(k, carry):
        pl.semaphore_signal(
            barrier, inc=1, device_id={"brick": lax.rem(brick + k, peers)}, device_id_type=MESH
        )
        return carry

    lax.fori_loop(1, peers, greet, 0)
    for k in range(1, modes):
        pl.semaphore_signal(
            barrier, inc=1, device_id={"mode": lax.rem(mode + k, modes)}, device_id_type=MESH
        )
    proj[slots] = jnp.zeros(proj.shape[1:], BF)
    ray[BLK_DEV] = jnp.zeros(ray.shape[1:], BF)
    loads[0].wait()
    for u in range(views):
        gpart[:, u * bins : (u + 1) * bins] = dot(picked[...], basis[u]).astype(BF)
    loads[1].wait()

    def round_low(i, carry):
        low[aligned(i, tile), :] = coef[aligned(i, tile), :].astype(BF)
        return carry

    lax.fori_loop(0, voxels // tile, round_low, 0)
    pl.semaphore_wait(barrier, peers - 1 + modes - 1)

    for k in range(1, modes):
        peer = lax.rem(mode + k, modes)
        to_mode(gpart.at[aligned(peer, share)], grecv.at[k - 1], gs_sem.at[k], gr_sem.at[k], peer)
    to_bricks(lambda peer: label_out.at[peer], label_in.at[brick], 0)
    pltpu.make_async_copy(label_out.at[brick], label_in.at[brick], local_sem.at[0]).start()

    def partial_pattern(v, slot, m):
        def body(i, carry):
            rows = aligned(i, tile)
            value = dot(low[rows, :], basis[v, :, aligned(m, mine)])
            if slot is None:
                pattern[v, rows, :] = value
            else:
                qsend[v, slot, rows, :] = value.astype(BF)
            return carry

        lax.fori_loop(0, voxels // tile, body, 0)

    lower, upper = pl.ds(0, half), pl.ds(half, half)

    def scatter_start(v):
        partial_pattern(v, 0, far)
        to_mode(qsend.at[v, 0, upper], qrel.at[v, 0], qs_sem.at[v, 0], qr_sem.at[v, 0], right)
        to_mode(qsend.at[v, 0, lower], qrel.at[v, 1], qs_sem.at[v, 1], qr_sem.at[v, 1], left)
        partial_pattern(v, 1, right)
        to_mode(
            qsend.at[v, 1, lower], qrecv.at[v, 0, lower], qs_sem.at[v, 2], qr_sem.at[v, 2], right
        )
        partial_pattern(v, 2, left)
        to_mode(
            qsend.at[v, 2, upper], qrecv.at[v, 1, upper], qs_sem.at[v, 3], qr_sem.at[v, 3], left
        )
        partial_pattern(v, None, mode)

    def scatter_relay(v):
        for k, (slot, start, part, peer) in enumerate(((1, half, upper, right), (2, 0, lower, left))):
            await_bytes(qrel.at[v, k], qr_sem.at[v, k])

            def body(i, carry, k=k, slot=slot, start=start):
                rows = pl.ds(pl.multiple_of(start + i * (tile // 2), tile // 2), tile // 2)
                given = qrel[v, k, aligned(i, tile // 2), :].astype(F32)
                qsend[v, slot, rows, :] = (qsend[v, slot, rows, :].astype(F32) + given).astype(BF)
                return carry

            lax.fori_loop(0, half // (tile // 2), body, 0)
            to_mode(
                qsend.at[v, slot, part], qrecv.at[v, k, part],
                qs_sem.at[v, 4 + k], qr_sem.at[v, 4 + k], peer,
            )

    def scatter_end(v):
        await_bytes(qrecv.at[v, 0, lower], qr_sem.at[v, 2])
        await_bytes(qrecv.at[v, 1, upper], qr_sem.at[v, 3])
        await_bytes(qrecv.at[v, 0, upper], qr_sem.at[v, 4])
        await_bytes(qrecv.at[v, 1, lower], qr_sem.at[v, 5])

        def body(i, carry):
            rows = aligned(i, tile)
            total = pattern[v, rows, :] + qrecv[v, 0, rows, :].astype(F32)
            total = total + qrecv[v, 1, rows, :].astype(F32)
            pattern[v, rows, :] = total
            qlow[v, rows, :] = total.astype(BF)
            return carry

        lax.fori_loop(0, voxels // tile, body, 0)

    scatter_start(0)
    own = aligned(mode, share)
    for k in range(1, modes):
        await_bytes(grecv.at[k - 1], gr_sem.at[k])
    total = gpart[own, :].astype(F32)
    for k in range(1, modes):
        total = total + grecv[k - 1].astype(F32)
    gram[aligned(brick, share), :] = total.astype(BF)
    to_bricks(lambda peer: gram.at[aligned(brick, share)], gram.at[aligned(brick, share)], 1)
    for m in range(modes):
        loads[4 + m].wait()
    for k in range(1, modes):
        peer = lax.rem(mode + k, modes)
        to_mode(chunk.at[peer], target.at[mode], ts_sem.at[k], tr_sem.at[k], peer)
    pltpu.make_async_copy(chunk.at[mode], target.at[mode], local_sem.at[1]).start()
    scatter_relay(0)
    scatter_start(1)

    await_bytes(label_in.at[pl.ds(0, peers - 1)], all_r.at[0])
    pltpu.make_async_copy(label_out.at[brick], label_in.at[brick], local_sem.at[0]).wait()
    table = pltpu.make_async_copy(label_in, label_s, local_sem.at[2])
    table.start()
    table.wait()
    group = 128 // ray_block

    def build(t, carry):
        row = lax.broadcasted_iota(jnp.int32, (rays, 128), 0)
        lane = lax.broadcasted_iota(jnp.int32, (rays, 128), 1)
        for v in range(views):
            want = jnp.zeros((rays, 128), jnp.int32)
            for g in range(group):
                entry = t * group + g
                label = label_s[entry // cap, 0, v * cap + entry % cap]
                inside = (lane >= g * ray_block) & (lane < (g + 1) * ray_block)
                want = jnp.where(inside, label * ray_block + lane - g * ray_block, want)
            select[v, :, aligned(t, 128)] = jnp.where(want == row, 1.0, 0.0).astype(BF)
        return carry

    lax.fori_loop(0, places_n // group, build, 0)

    def forward(s, v):
        def body(i, carry):
            value = dot(weight[v, aligned(i, rays), :], qlow[v]).astype(BF)
            proj[pl.ds(i * BLK_DEV, BLK_DEV)] = value.reshape(BLK_DEV, ray_block, mine)
            return carry

        lax.fori_loop(0, entries // rays, body, 0)
        if s:
            await_bytes(fsend.at[v, pl.ds(0, places_n - cap)], all_s.at[2 + v])

        def pack(i, carry):
            fsend[v, i] = proj[source[v, i]]
            return carry

        lax.fori_loop(0, places_n, pack, 0, unroll=8)
        where = pl.ds(brick * cap, cap)
        to_bricks(
            lambda peer: fsend.at[v, pl.ds(peer * cap, cap)], frecv.at[v, where], 2 + 4 * s + v
        )
        pltpu.make_async_copy(fsend.at[v, where], frecv.at[v, where], local_sem.at[3 + v]).start()

    def reflect(s, v):
        where = pl.ds(brick * cap, cap)
        await_bytes(frecv.at[v, pl.ds(0, places_n - cap)], all_r.at[2 + 4 * s + v])
        pltpu.make_async_copy(fsend.at[v, where], frecv.at[v, where], local_sem.at[3 + v]).wait()
        goal = jnp.concatenate([target[m, v] for m in range(modes)], 0)
        value = dot(select[v], frecv[v].reshape(places_n * ray_block, mine)) - goal
        if s:
            result[:, v] = value.reshape(modes, rays // modes, mine)
            await_bytes(bsend.at[v, pl.ds(0, places_n - cap)], all_s.at[4 + v])
        ray[pl.ds(0, BLK_DEV)] = value.astype(BF).reshape(BLK_DEV, ray_block, mine)

        def answer(p, carry):
            for c in range(cap):
                bsend[v, p * cap + c] = ray[label_s[p, 0, v * cap + c]]
            return carry

        lax.fori_loop(0, peers, answer, 0, unroll=4)
        to_bricks(
            lambda peer: bsend.at[v, pl.ds(peer * cap, cap)], brecv[v].at[where], 4 + 4 * s + v
        )
        pltpu.make_async_copy(bsend.at[v, where], brecv[v].at[where], local_sem.at[5 + v]).start()

    def adjoint(s, v):
        where = pl.ds(brick * cap, cap)
        await_bytes(brecv[v].at[pl.ds(0, places_n - cap)], all_r.at[4 + 4 * s + v])
        pltpu.make_async_copy(bsend.at[v, where], brecv[v].at[where], local_sem.at[5 + v]).wait()

        def unpack(i, carry):
            back[i] = brecv[v][places[v, i]]
            return carry

        lax.fori_loop(0, slots, unpack, 0, unroll=8 if slots % 8 == 0 else 1)

        def turn(i, carry):
            piece = back[pl.ds(i * BLK_DEV, BLK_DEV)].reshape(rays, mine).astype(F32)
            back_t[:, aligned(i, rays)] = piece.T.astype(BF)
            return carry

        lax.fori_loop(0, entries // rays, turn, 0)

        def body(j, carry):
            cols = aligned(j, tile)
            change[s, v, aligned(mode, mine), cols] = dot(back_t[...], weight[v, :, cols]).astype(BF)
            return carry

        lax.fori_loop(0, voxels // tile, body, 0)
        for k, (skip, peer) in enumerate(((hm, right), (0, right), (0, left), (hm, left))):
            part = change.at[s, v, pl.ds(pl.multiple_of(mode * mine + skip, hm), hm)]
            to_mode(part, part, as_sem.at[s, v, k], ar_sem.at[s, v, k], peer)

    def gather_relay(s, v):
        for k, (giver, skip, peer) in enumerate(((left, hm, right), (right, 0, left))):
            part = change.at[s, v, pl.ds(pl.multiple_of(giver * mine + skip, hm), hm)]
            await_bytes(part, ar_sem.at[s, v, 2 * k])
            to_mode(part, part, as_sem.at[s, v, 4 + k], ar_sem.at[s, v, 4 + k], peer)

    def gather_end(s, v):
        for k in (1, 3, 4, 5):
            await_bytes(change.at[s, v, pl.ds(0, hm)], ar_sem.at[s, v, k])

    def renew(u):
        def body(j, carry):
            cols = aligned(j, tile)
            step = dot(gram[:, u * bins : (u + 1) * bins], change[0, u, :, cols]).T
            for v in range(views):
                value = pattern[v, cols, :] - LEARN_RATE * step[:, v * mine : (v + 1) * mine]
                pattern[v, cols, :] = value
                if u == views - 1:
                    qlow[v, cols, :] = value.astype(BF)
            return carry

        lax.fori_loop(0, voxels // tile, body, 0)

    def update(s, us, out):
        def body(j, carry):
            cols = aligned(j, tile)
            step = sum(dot(basis[u], change[s, u, :, cols]) for u in us).T
            coef[cols, :] = coef[cols, :] - LEARN_RATE * step
            if out:
                pltpu.make_async_copy(
                    coef.at[cols], coeffs_out.at[cols], load_sem.at[j]
                ).start()
            return carry

        lax.fori_loop(0, voxels // tile, body, 0)

    scatter_end(0)
    loads[2].wait()
    forward(0, 0)
    scatter_relay(1)
    for k in range(1, modes):
        await_bytes(target.at[0], tr_sem.at[k])
    pltpu.make_async_copy(chunk.at[mode], target.at[mode], local_sem.at[1]).wait()
    reflect(0, 0)
    scatter_end(1)
    loads[3].wait()
    forward(0, 1)
    adjoint(0, 0)
    reflect(0, 1)
    gather_relay(0, 0)
    await_bytes(gram.at[pl.ds(0, gram.shape[0] - share)], all_r.at[1])
    gather_end(0, 0)
    renew(0)
    adjoint(0, 1)
    gather_relay(0, 1)
    gather_end(0, 1)
    renew(1)
    forward(1, 0)
    forward(1, 1)
    update(0, range(views), False)
    reflect(1, 0)
    reflect(1, 1)
    for k in range(1, modes):
        peer = lax.rem(mode + k, modes)
        to_mode(result.at[peer], collected.at[mode], rs_sem.at[k], rr_sem.at[k], peer)
    pltpu.make_async_copy(result.at[mode], collected.at[mode], local_sem.at[7]).start()
    adjoint(1, 0)
    gather_relay(1, 0)
    adjoint(1, 1)
    gather_end(1, 0)
    update(1, (0,), False)
    gather_relay(1, 1)
    for k in range(1, modes):
        await_bytes(collected.at[0], rr_sem.at[k])
    pltpu.make_async_copy(result.at[mode], collected.at[mode], local_sem.at[7]).wait()
    writes = [
        pltpu.make_async_copy(
            collected.at[m], residual_out.at[:, :, pl.ds(m * mine, mine)], load_sem.at[4 + m]
        )
        for m in range(modes)
    ]
    for write in writes:
        write.start()
    gather_end(1, 1)
    update(1, (1,), True)

    for k in range(1, modes):
        await_bytes(grecv.at[0], gs_sem.at[k])
        await_bytes(chunk.at[0], ts_sem.at[k])
        await_bytes(result.at[0], rs_sem.at[k])
    for v in range(views):
        for k in range(6):
            await_bytes(qrel.at[0, 0], qs_sem.at[v, k])
            for s in range(2):
                await_bytes(change.at[0, 0, pl.ds(0, hm)], as_sem.at[s, v, k])
        await_bytes(fsend.at[v, pl.ds(0, places_n - cap)], all_s.at[6 + v])
        await_bytes(bsend.at[v, pl.ds(0, places_n - cap)], all_s.at[8 + v])
    await_bytes(label_in.at[pl.ds(0, peers - 1)], all_s.at[0])
    await_bytes(gram.at[pl.ds(0, gram.shape[0] - share)], all_s.at[1])
    for write in writes:
        write.wait()

    def drain(j, carry):
        cols = aligned(j, tile)
        pltpu.make_async_copy(coef.at[cols], coeffs_out.at[cols], load_sem.at[j]).wait()
        return carry

    lax.fori_loop(0, voxels // tile, drain, 0)


def shards(coeffs, weights, owners, offsets, basis, measured):
    peers, modes = lax.axis_size("brick"), lax.axis_size("mode")
    views, slots, ray_block, voxels = weights.shape
    cap = max(2, slots // peers + 1)
    here, bins = basis.shape[1:]
    mine = bins // modes
    places_n = peers * cap
    rays = BLK_DEV * ray_block
    brick = lax.axis_index("brick")

    source, places, labels = jax.vmap(lambda o, f: slot_tables(o, f, peers, cap))(
        owners[:, :, 0], offsets
    )
    labels = jnp.moveaxis(labels.reshape(views, peers, cap), 1, 0).reshape(peers, views * cap)
    labels = jnp.pad(labels, ((0, 0), (0, 128 - views * cap))).reshape(peers, 1, 128)

    share = views * mine // peers
    view_here, bin_here = (brick * share) // mine, (brick * share) % mine
    picked = lax.dynamic_index_in_dim(basis, view_here, 0, keepdims=False)
    picked = lax.dynamic_slice_in_dim(picked.reshape(here, modes, mine), bin_here, share, 2)
    picked = picked.reshape(here, modes * share).T

    smem = pl.BlockSpec(memory_space=pltpu.SMEM)
    vmem = pl.BlockSpec(memory_space=pltpu.VMEM)
    anywhere = pl.BlockSpec(memory_space=pl.ANY)
    dma = pltpu.SemaphoreType.DMA
    blocks = (views, places_n, ray_block, mine)
    coeffs, residual = pl.pallas_call(
        functools.partial(kernel, peers, modes, cap),
        out_shape=(
            jax.ShapeDtypeStruct(coeffs.shape, F32),
            jax.ShapeDtypeStruct(measured.shape, F32),
        ),
        in_specs=[smem, smem, vmem, vmem] + [anywhere] * 4,
        out_specs=(anywhere, anywhere),
        scratch_shapes=[
            pltpu.VMEM(coeffs.shape, F32),
            pltpu.VMEM(coeffs.shape, BF),
            pltpu.VMEM(basis.shape, BF),
            pltpu.VMEM((views, slots * ray_block, voxels), BF),
            pltpu.VMEM((modes, views, rays // modes, mine), F32),
            pltpu.VMEM((modes, views, rays // modes, mine), F32),
            pltpu.VMEM((views, 3, voxels, mine), BF),
            pltpu.VMEM((views, 2, voxels // 2, mine), BF),
            pltpu.VMEM((views, 2, voxels, mine), BF),
            pltpu.VMEM((views, voxels, mine), F32),
            pltpu.VMEM((views, voxels, mine), BF),
            pltpu.VMEM((slots + 1, ray_block, mine), BF),
            pltpu.VMEM(blocks, BF),
            pltpu.VMEM(blocks, BF),
            pltpu.VMEM((BLK_DEV + 1, ray_block, mine), BF),
            pltpu.VMEM(blocks, BF),
            pltpu.VMEM(blocks[1:], BF),
            pltpu.VMEM(blocks[1:], BF),
            pltpu.VMEM((slots, ray_block, mine), BF),
            pltpu.VMEM((mine, slots * ray_block), BF),
            pltpu.VMEM((2, views, bins, voxels), BF),
            pltpu.VMEM((views, rays, places_n * ray_block), BF),
            pltpu.VMEM((views * mine, views * bins), BF),
            pltpu.VMEM((modes * share, views * bins), BF),
            pltpu.VMEM((modes - 1, share, views * bins), BF),
            pltpu.VMEM((peers, 1, 128), jnp.int32),
            pltpu.SMEM((peers, 1, 128), jnp.int32),
            pltpu.VMEM((modes, views, rays // modes, mine), F32),
            pltpu.VMEM((modes, views, rays // modes, mine), F32),
            dma((8,)),
            dma((8,)),
            dma((4,)),
            dma((4,)),
            dma((4,)),
            dma((4,)),
            dma((2, 6)),
            dma((2, 6)),
            dma((2, 2, 6)),
            dma((2, 2, 6)),
            dma((4,)),
            dma((4,)),
            dma((10,)),
            dma((10,)),
        ],
        compiler_params=pltpu.CompilerParams(
            collective_id=0, has_side_effects=True, vmem_limit_bytes=67043328
        ),
    )(source, places, labels, picked, coeffs, weights.reshape(views, -1, voxels), basis, measured)
    return coeffs, residual


def solution(mesh):
    return jax.shard_map(
        shards,
        mesh=mesh,
        in_specs=(
            P("brick", "mode"),
            P(None, "brick", None, None),
            P(None, "brick", None),
            P(None, "brick"),
            P(None, "mode", None),
            P(None, ("brick", "mode"), None),
        ),
        out_specs=(P("brick", "mode"), P(None, ("brick", "mode"), None)),
        check_vma=False,
    )
```

profile of v0, /device:TPU:1, one launch (start us, length us, event | category | flops | bytes accessed | tf_op | source)
XLA Modules:
  0.0 219.9 jit_solution(14021290242310264807)
XLA Ops:
  0.7 0.7 broadcast_add_fusion.1
  1.4 0.9 convert_reduce_fusion
  2.3 0.7 multiply_add_fusion.places
  3.0 0.0 copy-start.1
  3.0 0.1 select_reduce_fusion
  3.1 0.6 broadcast_add_fusion
  3.7 0.0 copy-done.1
  3.7 0.1 add.44
  3.8 0.1 copy.13
  3.9 0.1 copy.14
  4.0 0.6 pad.4
  4.6 1.5 constant_dynamic-slice_fusion
  6.1 0.7 copy.16
  6.8 0.7 constant_dynamic-slice_fusion.1
  7.5 207.8 %shard_map.77 = (f32[1024,768]{1,0:T(8,128)}, f32[2,64,1024]{2,1,0:T(8,128)}) custom-call(s32[2,64]{1,0:T(2,128)} %get-tuple-element.5.source, s32[2,48]{1,0:T(2,128)} %copy-done.1, s32[32,1,128]{2,1,0:T(1,128)} %bitcast.13, bf16[64,768]{1,0:T(8,128)(2,1)} %bitcast.11, f32[1024,768]{1,0:T(8,128)} %coeffs_hbm.1, bf16[2,1536,1024]{2,1,0:T(8,128)(2,1)} %bitcast.9, ...), custom_call_target="tpu_custom_call" | custom-call | tf_op jit(solution)/shard_map/pallas_call | solution.py:484
  215.3 0.0 copy-start
  215.3 3.8 %copy.19 = f32[1024,768]{1,0:T(8,128)} copy(f32[1024,768]{1,0:T(8,128)} %get-tuple-element.8) | data formatting | bytes 6291456
  219.1 0.0 copy-done
  219.1 0.8 copy.20
  (2 shorter events, 0.0 us)
Async XLA Ops:
  3.0 0.7 copy-start.1
  215.3 3.8 %copy-start = (f32[2,64,1024]{2,1,0:T(8,128)S(1)}, f32[2,64,1024]{2,1,0:T(8,128)}, u32[]{:S(2)}) copy-start(f32[2,64,1024]{2,1,0:T(8,128)} %get-tuple-element.9) | copy-start | bytes 1572868
where the time goes:
time: 223 us; the launch traced here: 220 us
  Pallas kernels  208 us (93%)
  local copies, waits for them, and re-layouts  8.39 us (4%)
  other arithmetic  3.02 us (1%)
    pallas_call x1, Pallas kernels, shards(): pl.pallas_call(functools.partial(kernel, peers, modes, cap), out_shape=(j...  208 us
    unnamed x7, local copies, waits for them, and re-layouts  5.32 us

commit v1 on v0

v1 whole, which is shorter than its diff:
```python
import functools

import jax
import jax.numpy as jnp
from jax import lax
from jax.experimental import pallas as pl
from jax.experimental.pallas import tpu as pltpu
from jax.sharding import PartitionSpec as P

BLK_DEV = 8
LEARN_RATE = 0.2
BF = jnp.bfloat16
F32 = jnp.float32
MESH = pl.DeviceIdType.MESH


def dot(a, b):
    return jnp.dot(a, b, preferred_element_type=F32)


def slot_tables(owner_list, offset_list, peer_count, capacity):
    slots = owner_list.shape[0]
    order = jnp.arange(slots, dtype=jnp.int32)
    same = owner_list[:, None] == owner_list[None, :]
    earlier = jnp.sum((same & (order[None, :] < order[:, None])).astype(jnp.int32), 1)
    places = owner_list * capacity + earlier
    hits = places[None, :] == jnp.arange(peer_count * capacity, dtype=jnp.int32)[:, None]
    source = slots + jnp.sum(jnp.where(hits, order[None, :] - slots, 0), 1)
    labels = BLK_DEV + jnp.sum(jnp.where(hits, offset_list[None, :] - BLK_DEV, 0), 1)
    return source, places, labels


def kernel(
    peers,
    modes,
    cap,
    source,
    places,
    label_out,
    picked,
    coeffs_hbm,
    weights_hbm,
    basis_hbm,
    measured_hbm,
    coeffs_out,
    residual_out,
    coef,
    low,
    basis,
    weight,
    chunk,
    target,
    qsend,
    qrel,
    qrecv,
    pattern,
    qlow,
    proj,
    fsend,
    frecv,
    ray,
    bsend,
    brecv0,
    brecv1,
    brecv2,
    brecv3,
    back,
    back_t,
    change,
    select,
    gram,
    gpart,
    grecv,
    label_in,
    label_s,
    result,
    collected,
    load_sem,
    local_sem,
    gs_sem,
    gr_sem,
    ts_sem,
    tr_sem,
    qs_sem,
    qr_sem,
    as_sem,
    ar_sem,
    rs_sem,
    rr_sem,
    all_s,
    all_r,
    write_sem,
):
    brecv = (brecv0, brecv1, brecv2, brecv3)
    brick, mode = lax.axis_index("brick"), lax.axis_index("mode")
    right, left, far = [lax.rem(mode + k, modes) for k in (1, modes - 1, 2)]
    views, entries, voxels = weights_hbm.shape
    slots, ray_block = proj.shape[0] - 1, proj.shape[1]
    here, bins = basis.shape[1], basis.shape[2]
    mine = bins // modes
    places_n = peers * cap
    rays = BLK_DEV * ray_block
    tile = min(256, voxels)
    width = mine // 2
    half, hm = voxels // 2, width // 2
    share = gpart.shape[0] // modes

    def aligned(i, n):
        return pl.ds(pl.multiple_of(i * n, n), n)

    def to_mode(src, dst, s, r, peer):
        copy = pltpu.make_async_remote_copy(
            src_ref=src, dst_ref=dst, send_sem=s, recv_sem=r,
            device_id={"mode": peer}, device_id_type=MESH,
        )
        copy.start()

    def await_bytes(ref, sem):
        pltpu.make_async_copy(ref, ref, sem).wait()

    def to_bricks(src_of, dst, index):
        def body(k, carry):
            peer = lax.rem(brick + k, peers)
            copy = pltpu.make_async_remote_copy(
                src_ref=src_of(peer), dst_ref=dst, send_sem=all_s.at[index],
                recv_sem=all_r.at[index], device_id={"brick": peer}, device_id_type=MESH,
            )
            copy.start()
            return carry

        lax.fori_loop(1, peers, body, 0)

    loads = [
        pltpu.make_async_copy(basis_hbm, basis, load_sem.at[0]),
        pltpu.make_async_copy(coeffs_hbm, coef, load_sem.at[1]),
        pltpu.make_async_copy(weights_hbm.at[0], weight.at[0], load_sem.at[2]),
        pltpu.make_async_copy(weights_hbm.at[1], weight.at[1], load_sem.at[3]),
    ]
    loads += [
        pltpu.make_async_copy(
            measured_hbm.at[:, :, pl.ds(m * mine, mine)], chunk.at[m], load_sem.at[4 + m]
        )
        for m in range(modes)
    ]
    for load in loads:
        load.start()
    barrier = pltpu.get_barrier_semaphore()

    def greet(k, carry):
        pl.semaphore_signal(
            barrier, inc=1, device_id={"brick": lax.rem(brick + k, peers)}, device_id_type=MESH
        )
        return carry

    lax.fori_loop(1, peers, greet, 0)
    for k in range(1, modes):
        pl.semaphore_signal(
            barrier, inc=1, device_id={"mode": lax.rem(mode + k, modes)}, device_id_type=MESH
        )
    proj[slots] = jnp.zeros(proj.shape[1:], BF)
    ray[BLK_DEV] = jnp.zeros(ray.shape[1:], BF)
    loads[0].wait()
    for u in range(views):
        gpart[:, u * bins : (u + 1) * bins] = dot(picked[...], basis[u]).astype(BF)
    loads[1].wait()

    def round_low(i, carry):
        low[aligned(i, tile), :] = coef[aligned(i, tile), :].astype(BF)
        return carry

    lax.fori_loop(0, voxels // tile, round_low, 0)
    lower, upper = pl.ds(0, half), pl.ds(half, half)

    def partial_patterns(v):
        def body(i, carry):
            rows = aligned(i, tile)
            for slot, m in ((0, far), (1, right), (2, left)):
                value = dot(low[rows, :], basis[v, :, aligned(m, mine)]).astype(BF)
                for h in range(2):
                    qsend[v, slot, h, rows, :] = value[:, h * width : (h + 1) * width]
            return carry

        lax.fori_loop(0, voxels // tile, body, 0)

    def own_pattern(v):
        def body(i, carry):
            rows = aligned(i, tile)
            value = dot(low[rows, :], basis[v, :, aligned(mode, mine)])
            for h in range(2):
                pattern[2 * v + h, rows, :] = value[:, h * width : (h + 1) * width]
            return carry

        lax.fori_loop(0, voxels // tile, body, 0)

    def scatter_send(c):
        v, h = c // 2, c % 2
        for k, (slot, part, dst, peer) in enumerate(
            (
                (0, upper, qrel.at[c, 0], right),
                (0, lower, qrel.at[c, 1], left),
                (1, lower, qrecv.at[c, 0, lower], right),
                (2, upper, qrecv.at[c, 1, upper], left),
            )
        ):
            to_mode(qsend.at[v, slot, h, part], dst, qs_sem.at[c, k], qr_sem.at[c, k], peer)

    def scatter_relay(c):
        v, h = c // 2, c % 2
        for k, (slot, start, part, peer) in enumerate(((1, half, upper, right), (2, 0, lower, left))):
            await_bytes(qrel.at[c, k], qr_sem.at[c, k])

            def body(i, carry, k=k, slot=slot, start=start):
                rows = pl.ds(pl.multiple_of(start + i * (tile // 2), tile // 2), tile // 2)
                given = qrel[c, k, aligned(i, tile // 2), :].astype(F32)
                total = qsend[v, slot, h, rows, :].astype(F32) + given
                qsend[v, slot, h, rows, :] = total.astype(BF)
                return carry

            lax.fori_loop(0, half // (tile // 2), body, 0)
            to_mode(
                qsend.at[v, slot, h, part], qrecv.at[c, k, part],
                qs_sem.at[c, 4 + k], qr_sem.at[c, 4 + k], peer,
            )

    def scatter_end(c):
        for k, part in ((2, lower), (3, upper), (4, upper), (5, lower)):
            await_bytes(qrecv.at[c, 0, part], qr_sem.at[c, k])

        def body(i, carry):
            rows = aligned(i, tile)
            total = pattern[c, rows, :] + qrecv[c, 0, rows, :].astype(F32)
            total = total + qrecv[c, 1, rows, :].astype(F32)
            pattern[c, rows, :] = total
            qlow[c, rows, :] = total.astype(BF)
            return carry

        lax.fori_loop(0, voxels // tile, body, 0)

    def share_gram():
        own = aligned(mode, share)
        for k in range(1, modes):
            await_bytes(grecv.at[k - 1], gr_sem.at[k])
        total = gpart[own, :].astype(F32)
        for k in range(1, modes):
            total = total + grecv[k - 1].astype(F32)
        gram[aligned(brick, share), :] = total.astype(BF)
        rows = gram.at[aligned(brick, share)]

        def body(k, carry):
            peer = lax.rem(brick + 2 * k, peers)
            copy = pltpu.make_async_remote_copy(
                src_ref=rows, dst_ref=rows, send_sem=all_s.at[1],
                recv_sem=all_r.at[1], device_id={"brick": peer}, device_id_type=MESH,
            )
            copy.start()
            return carry

        lax.fori_loop(1, peers // 2, body, 0)

    def hand_gram():
        await_bytes(gram.at[pl.ds(0, (peers // 2 - 1) * share)], all_r.at[1])
        core = lax.rem(brick, 2)
        twin = brick + 1 - 2 * core

        def body(k, carry):
            rows = gram.at[aligned(2 * k + core, share)]
            copy = pltpu.make_async_remote_copy(
                src_ref=rows, dst_ref=rows, send_sem=all_s.at[2],
                recv_sem=all_r.at[2], device_id={"brick": twin}, device_id_type=MESH,
            )
            copy.start()
            return carry

        lax.fori_loop(0, peers // 2, body, 0)

    def share_measured(v):
        for k in range(1, modes):
            peer = lax.rem(mode + k, modes)
            to_mode(
                chunk.at[peer, v], target.at[mode, v], ts_sem.at[v, k], tr_sem.at[v, k], peer
            )
        pltpu.make_async_copy(chunk.at[mode, v], target.at[mode, v], local_sem.at[1 + v]).start()

    def measured_end(v):
        for k in range(1, modes):
            await_bytes(target.at[0, v], tr_sem.at[v, k])
        pltpu.make_async_copy(chunk.at[mode, v], target.at[mode, v], local_sem.at[1 + v]).wait()

    def share_result(v):
        for k in range(1, modes):
            peer = lax.rem(mode + k, modes)
            to_mode(
                result.at[peer, v], collected.at[mode, v], rs_sem.at[v, k], rr_sem.at[v, k], peer
            )
        pltpu.make_async_copy(
            result.at[mode, v], collected.at[mode, v], local_sem.at[1 + v]
        ).start()

    def result_end(v):
        for k in range(1, modes):
            await_bytes(collected.at[0, v], rr_sem.at[v, k])
        pltpu.make_async_copy(
            result.at[mode, v], collected.at[mode, v], local_sem.at[1 + v]
        ).wait()

    group = 128 // ray_block

    def build_select():
        await_bytes(label_in.at[pl.ds(0, peers - 1)], all_r.at[0])
        pltpu.make_async_copy(label_out.at[brick], label_in.at[brick], local_sem.at[0]).wait()
        table = pltpu.make_async_copy(label_in, label_s, local_sem.at[0])
        table.start()
        table.wait()

        def build(t, carry):
            row = lax.broadcasted_iota(jnp.int32, (rays, 128), 0)
            lane = lax.broadcasted_iota(jnp.int32, (rays, 128), 1)
            for v in range(views):
                want = jnp.zeros((rays, 128), jnp.int32)
                for g in range(group):
                    entry = t * group + g
                    label = label_s[entry // cap, 0, v * cap + entry % cap]
                    inside = (lane >= g * ray_block) & (lane < (g + 1) * ray_block)
                    want = jnp.where(inside, label * ray_block + lane - g * ray_block, want)
                select[v, :, aligned(t, 128)] = jnp.where(want == row, 1.0, 0.0).astype(BF)
            return carry

        lax.fori_loop(0, places_n // group, build, 0)

    own_slots = pl.ds(brick * cap, cap)
    others = pl.ds(0, places_n - cap)

    def forward(s, c):
        v = c // 2

        def body(i, carry):
            value = dot(weight[v, aligned(i, rays), :], qlow[c]).astype(BF)
            proj[pl.ds(i * BLK_DEV, BLK_DEV)] = value.reshape(BLK_DEV, ray_block, width)
            return carry

        lax.fori_loop(0, entries // rays, body, 0)
        if s:
            await_bytes(fsend.at[c, others], all_s.at[3 + c])

        def pack(i, carry):
            fsend[c, i] = proj[source[v, i]]
            return carry

        lax.fori_loop(0, places_n, pack, 0, unroll=8)
        to_bricks(
            lambda peer: fsend.at[c, pl.ds(peer * cap, cap)], frecv.at[c, own_slots], 3 + 4 * s + c
        )
        pltpu.make_async_copy(
            fsend.at[c, own_slots], frecv.at[c, own_slots], local_sem.at[3 + c]
        ).start()

    def reflect(s, c):
        v, h = c // 2, c % 2
        lanes = slice(h * width, (h + 1) * width)
        await_bytes(frecv.at[c, others], all_r.at[3 + 4 * s + c])
        pltpu.make_async_copy(
            fsend.at[c, own_slots], frecv.at[c, own_slots], local_sem.at[3 + c]
        ).wait()
        goal = jnp.concatenate([target[m, v, :, lanes] for m in range(modes)], 0)
        value = dot(select[v], frecv[c].reshape(places_n * ray_block, width)) - goal
        if s:
            result[:, v, :, lanes] = value.reshape(modes, rays // modes, width)
            await_bytes(bsend.at[c, others], all_s.at[11 + c])
        ray[pl.ds(0, BLK_DEV)] = value.astype(BF).reshape(BLK_DEV, ray_block, width)

        def answer(p, carry):
            for k in range(cap):
                bsend[c, p * cap + k] = ray[label_s[p, 0, v * cap + k]]
            return carry

        lax.fori_loop(0, peers, answer, 0, unroll=4)
        to_bricks(
            lambda peer: bsend.at[c, pl.ds(peer * cap, cap)], brecv[c].at[own_slots], 11 + 4 * s + c
        )
        pltpu.make_async_copy(
            bsend.at[c, own_slots], brecv[c].at[own_slots], local_sem.at[7 + c]
        ).start()

    def adjoint(s, c):
        v, h = c // 2, c % 2
        await_bytes(brecv[c].at[others], all_r.at[11 + 4 * s + c])
        pltpu.make_async_copy(
            bsend.at[c, own_slots], brecv[c].at[own_slots], local_sem.at[7 + c]
        ).wait()

        def unpack(i, carry):
            back[i] = brecv[c][places[v, i]]
            return carry

        lax.fori_loop(0, slots, unpack, 0, unroll=8)

        def turn(i, carry):
            piece = back[pl.ds(i * BLK_DEV, BLK_DEV)].reshape(rays, width).astype(F32)
            back_t[:, aligned(i, rays)] = piece.T.astype(BF)
            return carry

        lax.fori_loop(0, entries // rays, turn, 0)
        rows = pl.ds(pl.multiple_of(mode * mine + h * width, width), width)

        def body(j, carry):
            cols = aligned(j, tile)
            change[s, v, rows, cols] = dot(back_t[...], weight[v, :, cols]).astype(BF)
            return carry

        lax.fori_loop(0, voxels // tile, body, 0)
        for k, (skip, peer) in enumerate(((hm, right), (0, right), (0, left), (hm, left))):
            part = change.at[
                s, v, pl.ds(pl.multiple_of(mode * mine + h * width + skip, hm), hm)
            ]
            to_mode(part, part, as_sem.at[s, c, k], ar_sem.at[s, c, k], peer)

    def gather_relay(s, c):
        v, h = c // 2, c % 2
        for k, (giver, skip, peer) in enumerate(((left, hm, right), (right, 0, left))):
            part = change.at[
                s, v, pl.ds(pl.multiple_of(giver * mine + h * width + skip, hm), hm)
            ]
            await_bytes(part, ar_sem.at[s, c, 2 * k])
            to_mode(part, part, as_sem.at[s, c, 4 + k], ar_sem.at[s, c, 4 + k], peer)

    def gather_end(s, c):
        for k in (1, 3, 4, 5):
            await_bytes(change.at[s, c // 2, pl.ds(0, hm)], ar_sem.at[s, c, k])

    def renew(u):
        def body(j, carry):
            cols = aligned(j, tile)
            step = dot(gram[:, u * bins : (u + 1) * bins], change[0, u, :, cols]).T
            for c in range(2 * views):
                value = pattern[c, cols, :] - LEARN_RATE * step[:, c * width : (c + 1) * width]
                pattern[c, cols, :] = value
                if u == views - 1:
                    qlow[c, cols, :] = value.astype(BF)
            return carry

        lax.fori_loop(0, voxels // tile, body, 0)

    def update(s, us, out):
        def body(j, carry):
            cols = aligned(j, tile)
            step = sum(dot(basis[u], change[s, u, :, cols]) for u in us).T
            coef[cols, :] = coef[cols, :] - LEARN_RATE * step
            if out:
                pltpu.make_async_copy(
                    coef.at[cols], coeffs_out.at[cols], load_sem.at[j]
                ).start()
            return carry

        lax.fori_loop(0, voxels // tile, body, 0)

    partial_patterns(0)
    own_pattern(0)
    pl.semaphore_wait(barrier, peers - 1 + modes - 1)

    for k in range(1, modes):
        peer = lax.rem(mode + k, modes)
        to_mode(gpart.at[aligned(peer, share)], grecv.at[k - 1], gs_sem.at[k], gr_sem.at[k], peer)
    to_bricks(lambda peer: label_out.at[peer], label_in.at[brick], 0)
    pltpu.make_async_copy(label_out.at[brick], label_in.at[brick], local_sem.at[0]).start()
    scatter_send(0)
    share_gram()
    for m in range(modes):
        loads[4 + m].wait()
    scatter_relay(0)
    share_measured(0)
    scatter_send(1)
    partial_patterns(1)
    own_pattern(1)
    loads[2].wait()
    scatter_end(0)
    forward(0, 0)
    build_select()
    scatter_relay(1)
    scatter_send(2)
    measured_end(0)
    reflect(0, 0)
    scatter_end(1)
    forward(0, 1)
    scatter_relay(2)
    share_measured(1)
    scatter_send(3)
    loads[3].wait()
    scatter_end(2)
    forward(0, 2)
    scatter_relay(3)
    adjoint(0, 0)
    reflect(0, 1)
    scatter_end(3)
    forward(0, 3)
    gather_relay(0, 0)
    measured_end(1)
    reflect(0, 2)
    hand_gram()
    adjoint(0, 1)
    reflect(0, 3)
    gather_relay(0, 1)
    adjoint(0, 2)
    gather_end(0, 0)
    gather_end(0, 1)
    await_bytes(gram.at[pl.ds(0, peers // 2 * share)], all_r.at[2])
    renew(0)
    gather_relay(0, 2)
    adjoint(0, 3)
    gather_relay(0, 3)
    gather_end(0, 2)
    gather_end(0, 3)
    renew(1)
    forward(1, 0)
    forward(1, 1)
    update(0, range(views), False)
    reflect(1, 0)
    forward(1, 2)
    reflect(1, 1)
    forward(1, 3)
    share_result(0)
    adjoint(1, 0)
    reflect(1, 2)
    gather_relay(1, 0)
    adjoint(1, 1)
    reflect(1, 3)
    share_result(1)
    gather_relay(1, 1)
    adjoint(1, 2)
    gather_relay(1, 2)
    adjoint(1, 3)
    gather_end(1, 0)
    gather_end(1, 1)
    update(1, (0,), False)
    gather_relay(1, 3)
    writes = []
    for v in range(views):
        result_end(v)
        writes += [
            pltpu.make_async_copy(
                collected.at[m, v],
                residual_out.at[v, :, pl.ds(m * mine, mine)],
                write_sem.at[v, m],
            )
            for m in range(modes)
        ]
    for write in writes:
        write.start()
    gather_end(1, 2)
    gather_end(1, 3)
    update(1, (1,), True)

    for k in range(1, modes):
        await_bytes(grecv.at[0], gs_sem.at[k])
        for v in range(views):
            await_bytes(chunk.at[0, v], ts_sem.at[v, k])
            await_bytes(result.at[0, v], rs_sem.at[v, k])
    for c in range(2 * views):
        for k in range(6):
            await_bytes(qrel.at[0, 0], qs_sem.at[c, k])
            for s in range(2):
                await_bytes(change.at[0, 0, pl.ds(0, hm)], as_sem.at[s, c, k])
        await_bytes(fsend.at[c, others], all_s.at[7 + c])
        await_bytes(bsend.at[c, others], all_s.at[15 + c])
    await_bytes(label_in.at[pl.ds(0, peers - 1)], all_s.at[0])
    await_bytes(gram.at[pl.ds(0, (peers // 2 - 1) * share)], all_s.at[1])
    await_bytes(gram.at[pl.ds(0, peers // 2 * share)], all_s.at[2])
    for write in writes:
        write.wait()

    def drain(j, carry):
        cols = aligned(j, tile)
        pltpu.make_async_copy(coef.at[cols], coeffs_out.at[cols], load_sem.at[j]).wait()
        return carry

    lax.fori_loop(0, voxels // tile, drain, 0)


def shards(coeffs, weights, owners, offsets, basis, measured):
    peers, modes = lax.axis_size("brick"), lax.axis_size("mode")
    views, slots, ray_block, voxels = weights.shape
    cap = max(2, slots // peers + 1)
    here, bins = basis.shape[1:]
    mine = bins // modes
    places_n = peers * cap
    rays = BLK_DEV * ray_block
    brick = lax.axis_index("brick")

    source, places, labels = jax.vmap(lambda o, f: slot_tables(o, f, peers, cap))(
        owners[:, :, 0], offsets
    )
    labels = jnp.moveaxis(labels.reshape(views, peers, cap), 1, 0).reshape(peers, views * cap)
    labels = jnp.pad(labels, ((0, 0), (0, 128 - views * cap))).reshape(peers, 1, 128)

    share = views * mine // peers
    view_here, bin_here = (brick * share) // mine, (brick * share) % mine
    picked = lax.dynamic_index_in_dim(basis, view_here, 0, keepdims=False)
    picked = lax.dynamic_slice_in_dim(picked.reshape(here, modes, mine), bin_here, share, 2)
    picked = picked.reshape(here, modes * share).T

    smem = pl.BlockSpec(memory_space=pltpu.SMEM)
    vmem = pl.BlockSpec(memory_space=pltpu.VMEM)
    anywhere = pl.BlockSpec(memory_space=pl.ANY)
    dma = pltpu.SemaphoreType.DMA
    chunks, width = 2 * views, mine // 2
    block = (places_n, ray_block, width)
    coeffs, residual = pl.pallas_call(
        functools.partial(kernel, peers, modes, cap),
        out_shape=(
            jax.ShapeDtypeStruct(coeffs.shape, F32),
            jax.ShapeDtypeStruct(measured.shape, F32),
        ),
        in_specs=[smem, smem, vmem, vmem] + [anywhere] * 4,
        out_specs=(anywhere, anywhere),
        scratch_shapes=[
            pltpu.VMEM(coeffs.shape, F32),
            pltpu.VMEM(coeffs.shape, BF),
            pltpu.VMEM(basis.shape, BF),
            pltpu.VMEM((views, slots * ray_block, voxels), BF),
            pltpu.VMEM((modes, views, rays // modes, mine), F32),
            pltpu.VMEM((modes, views, rays // modes, mine), F32),
            pltpu.VMEM((views, 3, 2, voxels, width), BF),
            pltpu.VMEM((chunks, 2, voxels // 2, width), BF),
            pltpu.VMEM((chunks, 2, voxels, width), BF),
            pltpu.VMEM((chunks, voxels, width), F32),
            pltpu.VMEM((chunks, voxels, width), BF),
            pltpu.VMEM((slots + 1, ray_block, width), BF),
            pltpu.VMEM((chunks,) + block, BF),
            pltpu.VMEM((chunks,) + block, BF),
            pltpu.VMEM((BLK_DEV + 1, ray_block, width), BF),
            pltpu.VMEM((chunks,) + block, BF),
            pltpu.VMEM(block, BF),
            pltpu.VMEM(block, BF),
            pltpu.VMEM(block, BF),
            pltpu.VMEM(block, BF),
            pltpu.VMEM((slots, ray_block, width), BF),
            pltpu.VMEM((width, slots * ray_block), BF),
            pltpu.VMEM((2, views, bins, voxels), BF),
            pltpu.VMEM((views, rays, places_n * ray_block), BF),
            pltpu.VMEM((views * mine, views * bins), BF),
            pltpu.VMEM((modes * share, views * bins), BF),
            pltpu.VMEM((modes - 1, share, views * bins), BF),
            pltpu.VMEM((peers, 1, 128), jnp.int32),
            pltpu.SMEM((peers, 1, 128), jnp.int32),
            pltpu.VMEM((modes, views, rays // modes, mine), F32),
            pltpu.VMEM((modes, views, rays // modes, mine), F32),
            dma((8,)),
            dma((11,)),
            dma((4,)),
            dma((4,)),
            dma((views, 4)),
            dma((views, 4)),
            dma((chunks, 6)),
            dma((chunks, 6)),
            dma((2, chunks, 6)),
            dma((2, chunks, 6)),
            dma((views, 4)),
            dma((views, 4)),
            dma((19,)),
            dma((19,)),
            dma((views, 4)),
        ],
        compiler_params=pltpu.CompilerParams(
            collective_id=0, has_side_effects=True, vmem_limit_bytes=67043328
        ),
    )(source, places, labels, picked, coeffs, weights.reshape(views, -1, voxels), basis, measured)
    return coeffs, residual


def solution(mesh):
    return jax.shard_map(
        shards,
        mesh=mesh,
        in_specs=(
            P("brick", "mode"),
            P(None, "brick", None, None),
            P(None, "brick", None),
            P(None, "brick"),
            P(None, "mode", None),
            P(None, ("brick", "mode"), None),
        ),
        out_specs=(P("brick", "mode"), P(None, ("brick", "mode"), None)),
        check_vma=False,
    )
```

time: 223 us -> 187 us (0.84); the launches traced: 220 us -> 186 us
  Pallas kernels: 208 us -> 174 us
    pallas_call x1, Pallas kernels: 208 us -> 174 us  [shards(): pl.pallas_call(functools.partial(kernel, peers, modes, cap), out_shape=(j...]
where the time goes in v1:
time: 187 us; the launch traced here: 186 us
  Pallas kernels  174 us (93%)
  local copies, waits for them, and re-layouts  8.39 us (4%)
  other arithmetic  3.02 us (2%)
    pallas_call x1, Pallas kernels, shards(): pl.pallas_call(functools.partial(kernel, peers, modes, cap), out_shape=(j...  174 us
    unnamed x7, local copies, waits for them, and re-layouts  5.32 us

profile of v1, /device:TPU:1, one launch (start us, length us, event | category | flops | bytes accessed | tf_op | source)
XLA Modules:
  0.0 186.3 jit_solution(8513536915122846499)
XLA Ops:
  0.7 0.7 broadcast_add_fusion.1
  1.4 0.9 convert_reduce_fusion
  2.3 0.7 multiply_add_fusion.places
  3.0 0.0 copy-start.1
  3.0 0.1 select_reduce_fusion
  3.1 0.6 broadcast_add_fusion
  3.7 0.0 copy-done.1
  3.7 0.1 add.44
  3.8 0.1 copy.13
  3.9 0.1 copy.14
  4.0 0.6 pad.4
  4.6 1.5 constant_dynamic-slice_fusion
  6.1 0.7 copy.16
  6.8 0.7 constant_dynamic-slice_fusion.1
  7.5 174.2 %shard_map.77 = (f32[1024,768]{1,0:T(8,128)}, f32[2,64,1024]{2,1,0:T(8,128)}) custom-call(s32[2,64]{1,0:T(2,128)} %get-tuple-element.5.source, s32[2,48]{1,0:T(2,128)} %copy-done.1, s32[32,1,128]{2,1,0:T(1,128)} %bitcast.13, bf16[64,768]{1,0:T(8,128)(2,1)} %bitcast.11, f32[1024,768]{1,0:T(8,128)} %coeffs_hbm.1, bf16[2,1536,1024]{2,1,0:T(8,128)(2,1)} %bitcast.9, ...), custom_call_target="tpu_custom_call" | custom-call | tf_op jit(solution)/shard_map/pallas_call | solution.py:606
  181.7 0.0 copy-start
  181.7 3.8 %copy.19 = f32[1024,768]{1,0:T(8,128)} copy(f32[1024,768]{1,0:T(8,128)} %get-tuple-element.8) | data formatting | bytes 6291456
  185.5 0.0 copy-done
  185.6 0.8 copy.20
  (2 shorter events, 0.0 us)
Async XLA Ops:
  3.0 0.7 copy-start.1
  181.7 3.8 %copy-start = (f32[2,64,1024]{2,1,0:T(8,128)S(1)}, f32[2,64,1024]{2,1,0:T(8,128)}, u32[]{:S(2)}) copy-start(f32[2,64,1024]{2,1,0:T(8,128)} %get-tuple-element.9) | copy-start | bytes 1572868

commit v2 on v1

--- a/solution.py
+++ b/solution.py
@@ -18,26 +18,12 @@
     return jnp.dot(a, b, preferred_element_type=F32)
 
 
-def slot_tables(owner_list, offset_list, peer_count, capacity):
-    slots = owner_list.shape[0]
-    order = jnp.arange(slots, dtype=jnp.int32)
-    same = owner_list[:, None] == owner_list[None, :]
-    earlier = jnp.sum((same & (order[None, :] < order[:, None])).astype(jnp.int32), 1)
-    places = owner_list * capacity + earlier
-    hits = places[None, :] == jnp.arange(peer_count * capacity, dtype=jnp.int32)[:, None]
-    source = slots + jnp.sum(jnp.where(hits, order[None, :] - slots, 0), 1)
-    labels = BLK_DEV + jnp.sum(jnp.where(hits, offset_list[None, :] - BLK_DEV, 0), 1)
-    return source, places, labels
-
-
 def kernel(
     peers,
     modes,
     cap,
-    source,
-    places,
-    label_out,
-    picked,
+    owners,
+    offsets,
     coeffs_hbm,
     weights_hbm,
     basis_hbm,
@@ -90,6 +76,12 @@
     all_s,
     all_r,
     write_sem,
+    table,
+    table_s,
+    label_flat,
+    label_out,
+    column,
+    mlow,
 ):
     brecv = (brecv0, brecv1, brecv2, brecv3)
     brick, mode = lax.axis_index("brick"), lax.axis_index("mode")
@@ -101,7 +93,7 @@
     places_n = peers * cap
     rays = BLK_DEV * ray_block
     tile = min(256, voxels)
-    width = mine // 2
+    width, chunks = mine // 2, 2 * views
     half, hm = voxels // 2, width // 2
     share = gpart.shape[0] // modes
 
@@ -142,8 +134,8 @@
         )
         for m in range(modes)
     ]
-    for load in loads:
-        load.start()
+    loads[0].start()
+    loads[1].start()
     barrier = pltpu.get_barrier_semaphore()
 
     def greet(k, carry):
@@ -159,16 +151,69 @@
         )
     proj[slots] = jnp.zeros(proj.shape[1:], BF)
     ray[BLK_DEV] = jnp.zeros(ray.shape[1:], BF)
+
+    def grid(rows, cols, dim):
+        return lax.broadcasted_iota(jnp.int32, (rows, cols), dim)
+
+    entry, lane = grid(slots, 128, 0), grid(slots, 128, 1)
+    flat = jnp.full((peers, 128), BLK_DEV, jnp.int32)
+    table[...] = jnp.zeros(table.shape, jnp.int32)
+    for v in range(views):
+        square = grid(slots, slots, 0) == grid(slots, slots, 1)
+        owner = jnp.sum(jnp.where(square, owners[v], 0), 1, keepdims=True)
+        owner_row = jnp.sum(jnp.where(entry == lane, owner, 0), 0, keepdims=True)
+        earlier = (owner == owner_row) & (lane < entry)
+        place = owner * cap + jnp.sum(jnp.where(earlier, 1, 0), 1, keepdims=True)
+        place_row = jnp.sum(jnp.where(entry == lane, place + 1, 0), 0, keepdims=True) - 1
+        offset = jnp.sum(jnp.where(square, offsets[v : v + 1, :], 0), 1, keepdims=True)
+        offset_row = jnp.sum(jnp.where(entry == lane, offset, 0), 0, keepdims=True)
+        source = jnp.sum(jnp.where(place == lane, entry - slots, 0), 0, keepdims=True) + slots
+        table[v, 0:1, :] = source
+        table[v, 1:2, :] = place_row
+        for k in range(cap):
+            hit = place_row == grid(peers, 128, 0) * cap + k
+            label = jnp.sum(jnp.where(hit, offset_row - BLK_DEV, 0), 1, keepdims=True) + BLK_DEV
+            flat = jnp.where(grid(peers, 128, 1) == v * cap + k, label, flat)
+    label_flat[...] = flat
+
+    def spread_labels(i, carry):
+        label_out[i] = label_flat[pl.ds(i, 1), :]
+        return carry
+
+    lax.fori_loop(0, peers, spread_labels, 0)
+    pltpu.make_async_copy(table, table_s, local_sem.at[0]).start()
+
     loads[0].wait()
+    start = brick * share
+    view_here, bin_here = start // mine, lax.rem(start, mine)
+    window = bin_here // 128
+    picked = []
+    for m in range(modes):
+        lanes = pl.ds(pl.multiple_of(m * mine + window * 128, 128), 128)
+        column[m] = basis[view_here, :, lanes].astype(F32).T.astype(BF)
+        rows = pl.ds(pl.multiple_of(lax.rem(bin_here, 128), share), share)
+        picked.append(column[m, rows, :])
+    picked = jnp.concatenate(picked, 0)
+    def half_basis(u, h):
+        return jnp.concatenate(
+            [basis[u, :, m * mine + h * width : m * mine + (h + 1) * width] for m in range(modes)], 1
+        )
+
     for u in range(views):
-        gpart[:, u * bins : (u + 1) * bins] = dot(picked[...], basis[u]).astype(BF)
+        for h in range(2):
+            at = u * bins + h * bins // 2
+            gpart[:, at : at + bins // 2] = dot(picked, half_basis(u, h)).astype(BF)
     loads[1].wait()
+    for load in loads[2:]:
+        load.start()
+    pltpu.make_async_copy(table, table_s, local_sem.at[0]).wait()
 
     def round_low(i, carry):
         low[aligned(i, tile), :] = coef[aligned(i, tile), :].astype(BF)
         return carry
 
     lax.fori_loop(0, voxels // tile, round_low, 0)
+
     lower, upper = pl.ds(0, half), pl.ds(half, half)
 
     def partial_patterns(v):
@@ -277,14 +322,14 @@
         for k in range(1, modes):
             peer = lax.rem(mode + k, modes)
             to_mode(
-                chunk.at[peer, v], target.at[mode, v], ts_sem.at[v, k], tr_sem.at[v, k], peer
+                mlow.at[peer, v], target.at[mode, v], ts_sem.at[v, k], tr_sem.at[v, k], peer
             )
-        pltpu.make_async_copy(chunk.at[mode, v], target.at[mode, v], local_sem.at[1 + v]).start()
+        pltpu.make_async_copy(mlow.at[mode, v], target.at[mode, v], local_sem.at[1 + v]).start()
 
     def measured_end(v):
         for k in range(1, modes):
             await_bytes(target.at[0, v], tr_sem.at[v, k])
-        pltpu.make_async_copy(chunk.at[mode, v], target.at[mode, v], local_sem.at[1 + v]).wait()
+        pltpu.make_async_copy(mlow.at[mode, v], target.at[mode, v], local_sem.at[1 + v]).wait()
 
     def share_result(v):
         for k in range(1, modes):
@@ -308,9 +353,9 @@
     def build_select():
         await_bytes(label_in.at[pl.ds(0, peers - 1)], all_r.at[0])
         pltpu.make_async_copy(label_out.at[brick], label_in.at[brick], local_sem.at[0]).wait()
-        table = pltpu.make_async_copy(label_in, label_s, local_sem.at[0])
-        table.start()
-        table.wait()
+        lookup = pltpu.make_async_copy(label_in, label_s, local_sem.at[0])
+        lookup.start()
+        lookup.wait()
 
         def build(t, carry):
             row = lax.broadcasted_iota(jnp.int32, (rays, 128), 0)
@@ -343,7 +388,7 @@
             await_bytes(fsend.at[c, others], all_s.at[3 + c])
 
         def pack(i, carry):
-            fsend[c, i] = proj[source[v, i]]
+            fsend[c, i] = proj[table_s[v, 0, i]]
             return carry
 
         lax.fori_loop(0, places_n, pack, 0, unroll=8)
@@ -362,10 +407,11 @@
             fsend.at[c, own_slots], frecv.at[c, own_slots], local_sem.at[3 + c]
         ).wait()
         goal = jnp.concatenate([target[m, v, :, lanes] for m in range(modes)], 0)
-        value = dot(select[v], frecv[c].reshape(places_n * ray_block, width)) - goal
+        value = dot(select[v], frecv[c].reshape(places_n * ray_block, width))
         if s:
             result[:, v, :, lanes] = value.reshape(modes, rays // modes, width)
             await_bytes(bsend.at[c, others], all_s.at[11 + c])
+        value = value - goal.astype(F32)
         ray[pl.ds(0, BLK_DEV)] = value.astype(BF).reshape(BLK_DEV, ray_block, width)
 
         def answer(p, carry):
@@ -389,7 +435,7 @@
         ).wait()
 
         def unpack(i, carry):
-            back[i] = brecv[c][places[v, i]]
+            back[i] = brecv[c][table_s[v, 1, i]]
             return carry
 
         lax.fori_loop(0, slots, unpack, 0, unroll=8)
@@ -400,7 +446,7 @@
             return carry
 
         lax.fori_loop(0, entries // rays, turn, 0)
-        rows = pl.ds(pl.multiple_of(mode * mine + h * width, width), width)
+        rows = aligned(h * modes + mode, width)
 
         def body(j, carry):
             cols = aligned(j, tile)
@@ -410,7 +456,7 @@
         lax.fori_loop(0, voxels // tile, body, 0)
         for k, (skip, peer) in enumerate(((hm, right), (0, right), (0, left), (hm, left))):
             part = change.at[
-                s, v, pl.ds(pl.multiple_of(mode * mine + h * width + skip, hm), hm)
+                s, v, pl.ds(pl.multiple_of((h * modes + mode) * width + skip, hm), hm)
             ]
             to_mode(part, part, as_sem.at[s, c, k], ar_sem.at[s, c, k], peer)
 
@@ -418,7 +464,7 @@
         v, h = c // 2, c % 2
         for k, (giver, skip, peer) in enumerate(((left, hm, right), (right, 0, left))):
             part = change.at[
-                s, v, pl.ds(pl.multiple_of(giver * mine + h * width + skip, hm), hm)
+                s, v, pl.ds(pl.multiple_of((h * modes + giver) * width + skip, hm), hm)
             ]
             await_bytes(part, ar_sem.at[s, c, 2 * k])
             to_mode(part, part, as_sem.at[s, c, 4 + k], ar_sem.at[s, c, 4 + k], peer)
@@ -427,23 +473,34 @@
         for k in (1, 3, 4, 5):
             await_bytes(change.at[s, c // 2, pl.ds(0, hm)], ar_sem.at[s, c, k])
 
-    def renew(u):
+    def renew(c, low_chunk, high_chunk):
+        u, h = c // 2, c % 2
+        part = pl.ds(h * bins // 2, bins // 2)
+        at = u * bins + h * bins // 2
+        rows = slice(low_chunk * width, high_chunk * width)
+
         def body(j, carry):
             cols = aligned(j, tile)
-            step = dot(gram[:, u * bins : (u + 1) * bins], change[0, u, :, cols]).T
-            for c in range(2 * views):
-                value = pattern[c, cols, :] - LEARN_RATE * step[:, c * width : (c + 1) * width]
-                pattern[c, cols, :] = value
-                if u == views - 1:
-                    qlow[c, cols, :] = value.astype(BF)
+            step = dot(gram[rows, at : at + bins // 2], change[0, u, part, cols]).T
+            for d in range(low_chunk, high_chunk):
+                i = d - low_chunk
+                value = pattern[d, cols, :] - LEARN_RATE * step[:, i * width : (i + 1) * width]
+                pattern[d, cols, :] = value
+                if c == chunks - 1:
+                    qlow[d, cols, :] = value.astype(BF)
             return carry
 
         lax.fori_loop(0, voxels // tile, body, 0)
 
-    def update(s, us, out):
+    def update(s, u, halves, out=False):
         def body(j, carry):
             cols = aligned(j, tile)
-            step = sum(dot(basis[u], change[s, u, :, cols]) for u in us).T
+            if len(halves) == 2:
+                lhs = jnp.concatenate([half_basis(u, h) for h in range(2)], 1)
+                step = dot(lhs, change[s, u, :, cols]).T
+            else:
+                part = pl.ds(halves[0] * bins // 2, bins // 2)
+                step = dot(half_basis(u, halves[0]), change[s, u, part, cols]).T
             coef[cols, :] = coef[cols, :] - LEARN_RATE * step
             if out:
                 pltpu.make_async_copy(
@@ -454,7 +511,6 @@
         lax.fori_loop(0, voxels // tile, body, 0)
 
     partial_patterns(0)
-    own_pattern(0)
     pl.semaphore_wait(barrier, peers - 1 + modes - 1)
 
     for k in range(1, modes):
@@ -463,18 +519,20 @@
     to_bricks(lambda peer: label_out.at[peer], label_in.at[brick], 0)
     pltpu.make_async_copy(label_out.at[brick], label_in.at[brick], local_sem.at[0]).start()
     scatter_send(0)
+    own_pattern(0)
+    partial_patterns(1)
+    own_pattern(1)
     share_gram()
     for m in range(modes):
         loads[4 + m].wait()
+    mlow[...] = chunk[...].astype(BF)
     scatter_relay(0)
     share_measured(0)
     scatter_send(1)
-    partial_patterns(1)
-    own_pattern(1)
+    build_select()
     loads[2].wait()
     scatter_end(0)
     forward(0, 0)
-    build_select()
     scatter_relay(1)
     scatter_send(2)
     measured_end(0)
@@ -501,58 +559,67 @@
     gather_relay(0, 1)
     adjoint(0, 2)
     gather_end(0, 0)
+    await_bytes(gram.at[pl.ds(0, peers // 2 * share)], all_r.at[2])
+    renew(0, 0, chunks)
     gather_end(0, 1)
-    await_bytes(gram.at[pl.ds(0, peers // 2 * share)], all_r.at[2])
-    renew(0)
+    renew(1, 0, chunks)
     gather_relay(0, 2)
     adjoint(0, 3)
     gather_relay(0, 3)
     gather_end(0, 2)
+    renew(2, 0, chunks)
     gather_end(0, 3)
-    renew(1)
+    renew(3, 0, 1)
     forward(1, 0)
+    renew(3, 1, chunks)
     forward(1, 1)
-    update(0, range(views), False)
+    update(0, 0, (0, 1))
     reflect(1, 0)
     forward(1, 2)
     reflect(1, 1)
     forward(1, 3)
     share_result(0)
+    update(0, 1, (0,))
     adjoint(1, 0)
     reflect(1, 2)
     gather_relay(1, 0)
+    update(0, 1, (1,))
     adjoint(1, 1)
     reflect(1, 3)
-    share_result(1)
     gather_relay(1, 1)
     adjoint(1, 2)
     gather_relay(1, 2)
     adjoint(1, 3)
     gather_end(1, 0)
     gather_end(1, 1)
-    update(1, (0,), False)
+    update(1, 0, (0, 1))
     gather_relay(1, 3)
+    share_result(1)
     writes = []
-    for v in range(views):
+
+    def write_residual(v):
         result_end(v)
-        writes += [
-            pltpu.make_async_copy(
+        collected[:, v] = collected[:, v] - chunk[:, v]
+        for m in range(modes):
+            write = pltpu.make_async_copy(
                 collected.at[m, v],
                 residual_out.at[v, :, pl.ds(m * mine, mine)],
                 write_sem.at[v, m],
             )
-            for m in range(modes)
-        ]
-    for write in writes:
-        write.start()
+            write.start()
+            writes.append(write)
+
+    write_residual(0)
     gather_end(1, 2)
+    update(1, 1, (0,))
     gather_end(1, 3)
-    update(1, (1,), True)
+    update(1, 1, (1,), True)
+    write_residual(1)
 
     for k in range(1, modes):
         await_bytes(grecv.at[0], gs_sem.at[k])
         for v in range(views):
-            await_bytes(chunk.at[0, v], ts_sem.at[v, k])
+            await_bytes(mlow.at[0, v], ts_sem.at[v, k])
             await_bytes(result.at[0, v], rs_sem.at[v, k])
     for c in range(2 * views):
         for k in range(6):
@@ -583,21 +650,8 @@
     mine = bins // modes
     places_n = peers * cap
     rays = BLK_DEV * ray_block
-    brick = lax.axis_index("brick")
-
-    source, places, labels = jax.vmap(lambda o, f: slot_tables(o, f, peers, cap))(
-        owners[:, :, 0], offsets
-    )
-    labels = jnp.moveaxis(labels.reshape(views, peers, cap), 1, 0).reshape(peers, views * cap)
-    labels = jnp.pad(labels, ((0, 0), (0, 128 - views * cap))).reshape(peers, 1, 128)
-
     share = views * mine // peers
-    view_here, bin_here = (brick * share) // mine, (brick * share) % mine
-    picked = lax.dynamic_index_in_dim(basis, view_here, 0, keepdims=False)
-    picked = lax.dynamic_slice_in_dim(picked.reshape(here, modes, mine), bin_here, share, 2)
-    picked = picked.reshape(here, modes * share).T
-
-    smem = pl.BlockSpec(memory_space=pltpu.SMEM)
+
     vmem = pl.BlockSpec(memory_space=pltpu.VMEM)
     anywhere = pl.BlockSpec(memory_space=pl.ANY)
     dma = pltpu.SemaphoreType.DMA
@@ -609,7 +663,7 @@
             jax.ShapeDtypeStruct(coeffs.shape, F32),
             jax.ShapeDtypeStruct(measured.shape, F32),
         ),
-        in_specs=[smem, smem, vmem, vmem] + [anywhere] * 4,
+        in_specs=[vmem, vmem] + [anywhere] * 4,
         out_specs=(anywhere, anywhere),
         scratch_shapes=[
             pltpu.VMEM(coeffs.shape, F32),
@@ -617,7 +671,7 @@
             pltpu.VMEM(basis.shape, BF),
             pltpu.VMEM((views, slots * ray_block, voxels), BF),
             pltpu.VMEM((modes, views, rays // modes, mine), F32),
-            pltpu.VMEM((modes, views, rays // modes, mine), F32),
+            pltpu.VMEM((modes, views, rays // modes, mine), BF),
             pltpu.VMEM((views, 3, 2, voxels, width), BF),
             pltpu.VMEM((chunks, 2, voxels // 2, width), BF),
             pltpu.VMEM((chunks, 2, voxels, width), BF),
@@ -658,11 +712,17 @@
             dma((19,)),
             dma((19,)),
             dma((views, 4)),
+            pltpu.VMEM((views, 8, 128), jnp.int32),
+            pltpu.SMEM((views, 8, 128), jnp.int32),
+            pltpu.VMEM((peers, 128), jnp.int32),
+            pltpu.VMEM((peers, 1, 128), jnp.int32),
+            pltpu.VMEM((modes, 128, here), BF),
+            pltpu.VMEM((modes, views, rays // modes, mine), BF),
         ],
         compiler_params=pltpu.CompilerParams(
             collective_id=0, has_side_effects=True, vmem_limit_bytes=67043328
         ),
-    )(source, places, labels, picked, coeffs, weights.reshape(views, -1, voxels), basis, measured)
+    )(owners.reshape(views, 1, slots), offsets, coeffs, weights.reshape(views, -1, voxels), basis, measured)
     return coeffs, residual
 
 

time: 187 us -> 179 us (0.957)
  local copies, waits for them, and re-layouts: 8.39 us -> 4.61 us
  other arithmetic: 3.02 us -> 0 us
    dynamic_slice x2 -> x0, local copies, waits for them, and re-layouts: 2.18 us -> none  [the longest x1 1.53 us: shards(): picked = lax.dynamic_index_in_dim(basis, view_here, 0, keepdims=False)]
    unnamed x7 -> x4, local copies, waits for them, and re-layouts: 5.32 us -> 4.61 us
where the time goes in v2:
time: 179 us; the launch traced here: 178 us
  Pallas kernels  173 us (97%)
  local copies, waits for them, and re-layouts  4.61 us (3%)
    pallas_call x1, Pallas kernels, shards(): pl.pallas_call(functools.partial(kernel, peers, modes, cap), out_shape=(j...  173 us
    unnamed x4, local copies, waits for them, and re-layouts  4.61 us

profile of v2, /device:TPU:1, one launch (start us, length us, event | category | flops | bytes accessed | tf_op | source)
XLA Modules:
  0.0 178.0 jit_solution(15040357813888024612)
XLA Ops:
  0.6 172.7 %shard_map.77 = (f32[1024,768]{1,0:T(8,128)}, f32[2,64,1024]{2,1,0:T(8,128)}) custom-call(s32[2,1,48]{2,1,0:T(1,128)} %bitcast.5, s32[2,48]{1,0:T(2,128)} %offsets.1, f32[1024,768]{1,0:T(8,128)} %coeffs_hbm.1, bf16[2,1536,1024]{2,1,0:T(8,128)(2,1)} %bitcast.4, bf16[2,768,1024]{2,1,0:T(8,128)(2,1)} %basis_hbm.1, f32[2,64,1024]{2,1,0:T(8,128)} %measured_hbm.1), custom_call_target="tpu_custom_call" | custom-call | tf_op jit(solution)/shard_map/pallas_call | solution.py:660
  173.3 0.0 copy-start
  173.3 3.8 %copy.11 = f32[1024,768]{1,0:T(8,128)} copy(f32[1024,768]{1,0:T(8,128)} %get-tuple-element.4) | data formatting | bytes 6291456
  177.2 0.0 copy-done
  177.2 0.8 copy.12
Async XLA Ops:
  173.3 3.8 %copy-start = (f32[2,64,1024]{2,1,0:T(8,128)S(1)}, f32[2,64,1024]{2,1,0:T(8,128)}, u32[]{:S(2)}) copy-start(f32[2,64,1024]{2,1,0:T(8,128)} %get-tuple-element.5) | copy-start | bytes 1572868

commit v3 on v2

--- a/solution.py
+++ b/solution.py
@@ -1,4 +1,5 @@
 import functools
+import math
 
 import jax
 import jax.numpy as jnp
@@ -16,6 +17,28 @@
 
 def dot(a, b):
     return jnp.dot(a, b, preferred_element_type=F32)
+
+
+def hand_over(coeffs, residual, coeffs_out, residual_out, rows, rays, in_sem, out_sem):
+    pieces = in_sem.shape[0] - 1
+    part = coeffs.shape[0] // pieces
+    moves = [(coeffs, rows, coeffs_out, pl.ds(i * part, part)) for i in range(pieces)]
+    moves.append((residual, rays, residual_out, pl.ds(0, residual.shape[0])))
+    ins = [
+        pltpu.make_async_copy(src.at[at], mid.at[at], in_sem.at[i])
+        for i, (src, mid, dst, at) in enumerate(moves)
+    ]
+    outs = [
+        pltpu.make_async_copy(mid.at[at], dst.at[at], out_sem.at[i])
+        for i, (src, mid, dst, at) in enumerate(moves)
+    ]
+    for move in ins:
+        move.start()
+    for first, second in zip(ins, outs):
+        first.wait()
+        second.start()
+    for move in outs:
+        move.wait()
 
 
 def kernel(
@@ -110,9 +133,18 @@
     def await_bytes(ref, sem):
         pltpu.make_async_copy(ref, ref, sem).wait()
 
+    side = math.isqrt(peers // 2)
+    deep = peers // (2 * side)
+
+    def partner(dz, dy, dc):
+        z = lax.rem(brick // (2 * side) + dz, deep)
+        y = lax.rem(lax.rem(brick // 2, side) + dy, side)
+        return (z * side + y) * 2 + lax.rem(lax.rem(brick, 2) + dc, 2)
+
     def to_bricks(src_of, dst, index):
         def body(k, carry):
-            peer = lax.rem(brick + k, peers)
+            q = lax.rem(k * 13, peers)
+            peer = partner(q // (2 * side), lax.rem(q // 2, side), lax.rem(q, 2))
             copy = pltpu.make_async_remote_copy(
                 src_ref=src_of(peer), dst_ref=dst, send_sem=all_s.at[index],
                 recv_sem=all_r.at[index], device_id={"brick": peer}, device_id_type=MESH,
@@ -292,7 +324,8 @@
         rows = gram.at[aligned(brick, share)]
 
         def body(k, carry):
-            peer = lax.rem(brick + 2 * k, peers)
+            q = lax.rem(k * 5, peers // 2)
+            peer = partner(q // side, lax.rem(q, side), 0)
             copy = pltpu.make_async_remote_copy(
                 src_ref=rows, dst_ref=rows, send_sem=all_s.at[1],
                 recv_sem=all_r.at[1], device_id={"brick": peer}, device_id_type=MESH,
@@ -723,7 +756,22 @@
             collective_id=0, has_side_effects=True, vmem_limit_bytes=67043328
         ),
     )(owners.reshape(views, 1, slots), offsets, coeffs, weights.reshape(views, -1, voxels), basis, measured)
-    return coeffs, residual
+    return pl.pallas_call(
+        hand_over,
+        out_shape=(
+            jax.ShapeDtypeStruct(coeffs.shape, F32),
+            jax.ShapeDtypeStruct(residual.shape, F32),
+        ),
+        in_specs=[anywhere, anywhere],
+        out_specs=(anywhere, anywhere),
+        scratch_shapes=[
+            pltpu.VMEM(coeffs.shape, F32),
+            pltpu.VMEM(residual.shape, F32),
+            dma((9,)),
+            dma((9,)),
+        ],
+        compiler_params=pltpu.CompilerParams(vmem_limit_bytes=67043328),
+    )(coeffs, residual)
 
 
 def solution(mesh):

time: 179 us -> 175 us (0.978)
  local copies, waits for them, and re-layouts: 4.61 us -> 0 us
    unnamed x4 -> x0, local copies, waits for them, and re-layouts: 4.61 us -> none
    pallas_call x1, Pallas kernels: 173 us -> 169 us  [shards(): pl.pallas_call(functools.partial(kernel, peers, modes, cap), out_shape=(j...]
    pallas_call x0 -> x1, Pallas kernels: none -> 3.15 us  [shards(): pl.pallas_call(hand_over, out_shape=(jax.ShapeDtypeStruct(coeffs.shape, F...]
where the time goes in v3:
time: 175 us; the launch traced here: 173 us
  Pallas kernels  172 us (98%)
    pallas_call x1, Pallas kernels, shards(): pl.pallas_call(functools.partial(kernel, peers, modes, cap), out_shape=(j...  169 us

profile of v3, /device:TPU:1, one launch (start us, length us, event | category | flops | bytes accessed | tf_op | source)
XLA Modules:
  0.0 172.9 jit_solution(4295462294256970430)
XLA Ops:
  0.6 169.0 %shard_map.77 = (f32[1024,768]{1,0:T(8,128)}, f32[2,64,1024]{2,1,0:T(8,128)}) custom-call(s32[2,1,48]{2,1,0:T(1,128)} %bitcast.5, s32[2,48]{1,0:T(2,128)} %offsets.1, f32[1024,768]{1,0:T(8,128)} %coeffs_hbm.1, bf16[2,1536,1024]{2,1,0:T(8,128)(2,1)} %bitcast.4, bf16[2,768,1024]{2,1,0:T(8,128)(2,1)} %basis_hbm.1, f32[2,64,1024]{2,1,0:T(8,128)} %measured_hbm.1), custom_call_target="tpu_custom_call" | custom-call | tf_op jit(solution)/shard_map/pallas_call | solution.py:693
  169.6 3.2 %shard_map.78 = (f32[1024,768]{1,0:T(8,128)}, f32[2,64,1024]{2,1,0:T(8,128)}) custom-call(f32[1024,768]{1,0:T(8,128)} %get-tuple-element.4.coeffs, f32[2,64,1024]{2,1,0:T(8,128)} %get-tuple-element.5.residual), custom_call_target="tpu_custom_call" | custom-call | tf_op jit(solution)/shard_map/pallas_call | solution.py:759

commit v4 on v3

--- a/solution.py
+++ b/solution.py
@@ -570,15 +570,15 @@
     scatter_send(2)
     measured_end(0)
     reflect(0, 0)
+    scatter_relay(2)
+    scatter_send(3)
     scatter_end(1)
     forward(0, 1)
-    scatter_relay(2)
     share_measured(1)
-    scatter_send(3)
     loads[3].wait()
     scatter_end(2)
+    scatter_relay(3)
     forward(0, 2)
-    scatter_relay(3)
     adjoint(0, 0)
     reflect(0, 1)
     scatter_end(3)

time: 175 us -> 174 us (level); the launches traced: 173 us -> 174 us
  no operation moved by 1% of the time
where the time goes in v4:
time: 174 us
  Pallas kernels  173 us (99%)
    pallas_call x1, Pallas kernels, shards(): pl.pallas_call(functools.partial(kernel, peers, modes, cap), out_shape=(j...  170 us

profile of v4, /device:TPU:1, one launch (start us, length us, event | category | flops | bytes accessed | tf_op | source)
XLA Modules:
  0.0 173.7 jit_solution(9552897576088730683)
XLA Ops:
  0.6 169.7 %shard_map.77 = (f32[1024,768]{1,0:T(8,128)}, f32[2,64,1024]{2,1,0:T(8,128)}) custom-call(s32[2,1,48]{2,1,0:T(1,128)} %bitcast.5, s32[2,48]{1,0:T(2,128)} %offsets.1, f32[1024,768]{1,0:T(8,128)} %coeffs_hbm.1, bf16[2,1536,1024]{2,1,0:T(8,128)(2,1)} %bitcast.4, bf16[2,768,1024]{2,1,0:T(8,128)(2,1)} %basis_hbm.1, f32[2,64,1024]{2,1,0:T(8,128)} %measured_hbm.1), custom_call_target="tpu_custom_call" | custom-call | tf_op jit(solution)/shard_map/pallas_call | solution.py:693
  170.4 3.2 %shard_map.78 = (f32[1024,768]{1,0:T(8,128)}, f32[2,64,1024]{2,1,0:T(8,128)}) custom-call(f32[1024,768]{1,0:T(8,128)} %get-tuple-element.4.coeffs, f32[2,64,1024]{2,1,0:T(8,128)} %get-tuple-element.5.residual), custom_call_target="tpu_custom_call" | custom-call | tf_op jit(solution)/shard_map/pallas_call | solution.py:759
